TPU v7x, 32 devices: a whole 2x2x4 slice. The times are simulated.
32 devices in a mesh: row: 4 (over z), col: 2 (over y), depth: 4 (over x, core).
Axes of the slice: x: 2, y: 2, z: 4, core: 2. Of those that a mesh axis runs over, the one named last changes fastest.
Arguments:
- factor: float32 [4096, 1536], P(('row', 'col', 'depth')), may hold values from -1 to 4, as said below
- update: float32 [4096, 256], P(('row', 'col', 'depth')), may hold values from -0.375 to 0.375
Outputs:
- new_factor: float32 [4096, 1536], P(('row', 'col', 'depth'))
- new_update: float32 [4096, 256], P(('row', 'col', 'depth'))
Inputs may be any that keep to these rules, and one draw needn't show every extreme that they name: `factor`: zero above the diagonal; each diagonal entry is 1 or more.
All inputs are finite; a program needn't handle non-finite values.
Results may differ from a plain program's by a relative error of at most 0.00013.
Values sent between devices are 32-bit elements; how exact they have to be, the bound alone decides.
A program may use at most 128 MiB of HBM per device.

v0:
```python
import jax
import jax.numpy as jnp
from jax import lax
from jax.sharding import PartitionSpec as P

B = 512
PANELS = 3


def spread(block, axis, owner):
    block = jnp.where(lax.axis_index(axis) == owner, block, jnp.zeros_like(block))
    return lax.psum(block, axis)


def transform(stacked):
    panel_width = stacked.shape[0]
    diag_block = stacked[:, :panel_width]
    v_block = stacked[:, panel_width:]
    update_rank = v_block.shape[1]
    gram_matrix = jnp.dot(stacked, stacked.T, precision=lax.Precision.HIGHEST)
    new_diag = jnp.linalg.cholesky(gram_matrix)
    leading = jax.scipy.linalg.solve_triangular(new_diag, stacked, lower=True)
    coupling = jax.scipy.linalg.solve_triangular(diag_block, v_block, lower=True)
    identity_k = jnp.eye(update_rank, dtype=jnp.float32)
    inner_gram = identity_k + jnp.dot(coupling.T, coupling, precision=lax.Precision.HIGHEST)
    lower_inner = jnp.linalg.cholesky(inner_gram)
    null_basis = jnp.concatenate([-coupling, identity_k], 0)
    second = jax.scipy.linalg.solve_triangular(lower_inner, null_basis.T, lower=True).T
    return jnp.concatenate([leading.T, second], 1)


def on_device(factor, update):
    rows_dev = factor.shape[0]
    row_ids = lax.axis_index(("row", "col", "depth")) * rows_dev + jnp.arange(
        rows_dev, dtype=jnp.int32
    )
    early_slabs = []
    for owner_index in range(PANELS):
        width = (owner_index + 1) * B
        early_slabs.append(
            (
                spread(factor[:, :width], ("row", "col"), owner_index),
                spread(update, ("row", "col"), owner_index),
            )
        )
    for panel_index in range(PANELS):
        panel_start = panel_index * B
        panel_cols = factor[:, panel_start : panel_start + B]
        stacked = jnp.concatenate([panel_cols, update], 1)
        slab_cols, slab_update = early_slabs[panel_index]
        current = jnp.concatenate([slab_cols[:, panel_start : panel_start + B], slab_update], 1)
        diag_rows = lax.all_gather(current, "depth", axis=0, tiled=True)
        rotation = transform(diag_rows)
        for later in range(panel_index + 1, PANELS):
            later_cols, later_update = early_slabs[later]
            joined = jnp.concatenate(
                [later_cols[:, panel_start : panel_start + B], later_update], 1
            )
            early_slabs[later] = (
                later_cols,
                jnp.dot(joined, rotation[:, B:], precision=lax.Precision.HIGHEST),
            )
        moved = jnp.dot(stacked, rotation, precision=lax.Precision.HIGHEST)
        col_ids = panel_start + jnp.arange(B, dtype=jnp.int32)
        new_cols = jnp.where(row_ids[:, None] >= col_ids[None, :], moved[:, :B], jnp.float32(0.0))
        update = jnp.where(row_ids[:, None] >= panel_start, moved[:, B:], update)
        factor = factor.at[:, panel_start : panel_start + B].set(new_cols)
    return (factor, update)


def solution(mesh):
    return jax.shard_map(
        on_device,
        mesh=mesh,
        in_specs=(P(("row", "col", "depth"), None), P(("row", "col", "depth"), None)),
        out_specs=(P(("row", "col", "depth"), None), P(("row", "col", "depth"), None)),
        check_vma=False,
    )
```

profile of v0, /device:TPU:0, one launch (start us, length us, event | category | flops | bytes accessed | tf_op | source)
XLA Modules:
  0.0 1116.5 jit_solution(5682356321159899076)
XLA Ops:
  11.8 103.0 %all-reduce.5.cloned.1.call-done = (f32[128,256]{1,0:T(8,128)}, f32[128,512]{1,0:T(8,128)}, f32[128,256]{1,0:T(8,128)}, f32[128,1024]{1,0:T(8,128)}, f32[128,256]{1,0:T(8,128)}, /*index=5*/f32[128,1536]{1,0:T(8,128)}) async-done(((f32[128,256]{1,0:T(8,128)}, f32[128,512]{1,0:T(8,128)}, f32[128,256]{1,0:T(8,128)}, f32[128,1024]{1,0:T(8,128)}, f32[128,256]{1,0:T(8,128)}, /*index=5*/f32[128,1536]{1,0:T(8,128)}), ...) | async-done | bytes 1966096 | tf_op jit(solution)/shard_map/psum | solution.py:12
  122.2 13.5 %all-gather.4.cloned.1.call-done = f32[512,768]{1,0:T(8,128)} async-done(((f32[128,768]{1,0:T(8,128)}), f32[512,768]{1,0:T(8,128)}) %all-gather.4.cloned.1.call-update) | async-done | bytes 1572880 | tf_op jit(solution)/shard_map/all_gather | solution.py:52
  138.2 11.6 %while.22 = (s32[]{:T(128)}, f32[512,512]{1,0:T(8,128)}, s32[4,2]{0,1:T(2,128)S(1)}, f32[4,128,128]{2,1,0:T(8,128)S(1)}, s32[]{:T(128)}) while((s32[]{:T(128)}, f32[512,512]{1,0:T(8,128)}, s32[4,2]{0,1:T(2,128)S(1)}, f32[4,128,128]{2,1,0:T(8,128)S(1)}, s32[]{:T(128)}) %tuple.194), condition=%wide.while_cond.4, body=%wide.while_body.4.sunk | while | flops 2 | bytes 131189 | solution.py:23
  149.8 39.5 %custom-call.57 = f32[4,128,128]{1,2,0:T(8,128)S(1)} custom-call(f32[4,128,128]{2,1,0:T(8,128)S(1)} %get-tuple-element.105), custom_call_target="InvertDiagBlocksLowerTriangular" | custom-call | tf_op jit(solution)/shard_map/jit(_solve_triangular)/triangular_solve | solution.py:23
  199.5 11.7 %cholesky.560 = f32[128,128]{1,0:T(8,128)S(1)} custom-call(f32[128,128]{1,0:T(8,128)S(1)} %cholesky.786), custom_call_target="Cholesky" | custom-call | tf_op jit(solution)/shard_map/jit(cholesky)/cholesky | solution.py:26
  212.0 9.8 custom-call.58
  224.6 12.1 %cholesky.570 = f32[128,128]{1,0:T(8,128)S(1)} custom-call(f32[128,128]{1,0:T(8,128)S(1)} %convolution_subtract_fusion.29), custom_call_target="Cholesky" | custom-call | tf_op jit(solution)/shard_map/jit(cholesky)/cholesky | solution.py:26
  240.9 5.6 while.23
  247.1 19.7 %custom-call.59 = f32[2,128,128]{1,2,0:T(8,128)S(1)} custom-call(f32[2,128,128]{2,1,0:T(8,128)S(1)} %get-tuple-element.106), custom_call_target="InvertDiagBlocksLowerTriangular" | custom-call | tf_op jit(solution)/shard_map/jit(_solve_triangular)/triangular_solve | solution.py:28
  270.4 3.7 fusion.236
  274.1 2.6 copy.4
  280.0 13.2 %cholesky.492 = f32[128,128]{1,0:T(8,128)} custom-call(f32[128,128]{1,0:T(8,128)} %cholesky.773), custom_call_target="Cholesky" | custom-call | tf_op jit(solution)/shard_map/jit(cholesky)/cholesky | solution.py:21
  297.2 11.3 %custom-call.53 = f32[1,128,128]{1,2,0:T(8,128)} custom-call(f32[1,128,128]{2,1,0:T(8,128)} %get-tuple-element.256), custom_call_target="InvertDiagBlocksLowerTriangular" | custom-call | tf_op jit(solution)/shard_map/jit(cholesky)/cholesky | solution.py:21
  313.0 13.3 %cholesky.511 = f32[128,128]{1,0:T(8,128)} custom-call(f32[128,128]{1,0:T(8,128)} %cholesky.777), custom_call_target="Cholesky" | custom-call | tf_op jit(solution)/shard_map/jit(cholesky)/cholesky | solution.py:21
  328.4 11.3 %custom-call.54 = f32[1,128,128]{1,2,0:T(8,128)} custom-call(f32[1,128,128]{2,1,0:T(8,128)} %get-tuple-element.253), custom_call_target="InvertDiagBlocksLowerTriangular" | custom-call | tf_op jit(solution)/shard_map/jit(cholesky)/cholesky | solution.py:21
  344.2 13.2 %cholesky.532 = f32[128,128]{1,0:T(8,128)} custom-call(f32[128,128]{1,0:T(8,128)} %cholesky.782), custom_call_target="Cholesky" | custom-call | tf_op jit(solution)/shard_map/jit(cholesky)/cholesky | solution.py:21
  359.3 11.5 %custom-call.55 = f32[1,128,128]{1,2,0:T(8,128)} custom-call(f32[1,128,128]{2,1,0:T(8,128)} %get-tuple-element.250), custom_call_target="InvertDiagBlocksLowerTriangular" | custom-call | tf_op jit(solution)/shard_map/jit(cholesky)/cholesky/custom-call.11 | solution.py:21
  374.6 13.2 %cholesky.545 = f32[128,128]{1,0:T(8,128)} custom-call(f32[128,128]{1,0:T(8,128)} %convolution_subtract_fusion.32), custom_call_target="Cholesky" | custom-call | tf_op jit(solution)/shard_map/jit(cholesky)/cholesky | solution.py:21
  398.1 13.6 %while.21 = (s32[]{:T(128)}, f32[512,512]{1,0:T(8,128)}, s32[4,2]{0,1:T(2,128)S(1)}, f32[4,128,128]{2,1,0:T(8,128)}, s32[]{:T(128)}) while((s32[]{:T(128)}, f32[512,512]{1,0:T(8,128)}, s32[4,2]{0,1:T(2,128)S(1)}, f32[4,128,128]{2,1,0:T(8,128)}, s32[]{:T(128)}) %tuple.230), condition=%wide.while_cond.3, body=%wide.while_body.3.sunk | while | flops 2 | bytes 132205 | solution.py:22
  398.7 2.8 bitcast_dynamic-update-slice_fusion.18
  402.1 2.8 bitcast_dynamic-update-slice_fusion.18
  405.5 2.8 bitcast_dynamic-update-slice_fusion.18
  408.9 2.8 bitcast_dynamic-update-slice_fusion.18
  411.7 40.7 %custom-call.56 = f32[4,128,128]{1,2,0:T(8,128)} custom-call(f32[4,128,128]{2,1,0:T(8,128)} %get-tuple-element.104), custom_call_target="InvertDiagBlocksLowerTriangular" | custom-call | tf_op jit(solution)/shard_map/jit(_solve_triangular)/triangular_solve | solution.py:22
  465.2 2.5 fusion
  471.6 4.3 all-gather.6.cloned.1.call-done
  475.9 2.5 slice_select_fusion.1
  478.4 11.6 %while.25 = (s32[]{:T(128)}, f32[512,512]{1,0:T(8,128)}, s32[4,2]{0,1:T(2,128)S(1)}, f32[4,128,128]{2,1,0:T(8,128)S(1)}, s32[]{:T(128)}) while((s32[]{:T(128)}, f32[512,512]{1,0:T(8,128)}, s32[4,2]{0,1:T(2,128)S(1)}, f32[4,128,128]{2,1,0:T(8,128)S(1)}, s32[]{:T(128)}) %tuple.231), condition=%wide.while_cond.4.clone, body=%wide.while_body.4.clone.sunk | while | flops 2 | bytes 131189 | solution.py:23
  490.0 39.5 %custom-call.64 = f32[4,128,128]{1,2,0:T(8,128)S(1)} custom-call(f32[4,128,128]{2,1,0:T(8,128)S(1)} %get-tuple-element.108), custom_call_target="InvertDiagBlocksLowerTriangular" | custom-call | tf_op jit(solution)/shard_map/jit(_solve_triangular)/triangular_solve | solution.py:23
  539.0 11.7 %cholesky.655 = f32[128,128]{1,0:T(8,128)S(1)} custom-call(f32[128,128]{1,0:T(8,128)S(1)} %cholesky.802), custom_call_target="Cholesky" | custom-call | tf_op jit(solution)/shard_map/jit(cholesky)/cholesky | solution.py:26
  551.3 10.4 custom-call.65
  563.9 12.1 %cholesky.665 = f32[128,128]{1,0:T(8,128)S(1)} custom-call(f32[128,128]{1,0:T(8,128)S(1)} %convolution_subtract_fusion.28), custom_call_target="Cholesky" | custom-call | tf_op jit(solution)/shard_map/jit(cholesky)/cholesky | solution.py:26
  580.2 5.3 while.26
  585.5 20.3 %custom-call.66 = f32[2,128,128]{1,2,0:T(8,128)} custom-call(f32[2,128,128]{2,1,0:T(8,128)S(1)} %get-tuple-element.109), custom_call_target="InvertDiagBlocksLowerTriangular" | custom-call | tf_op jit(solution)/shard_map/jit(_solve_triangular)/triangular_solve | solution.py:28
  609.3 2.7 fusion.237
  615.8 11.7 %cholesky.587 = f32[128,128]{1,0:T(8,128)S(1)} custom-call(f32[128,128]{1,0:T(8,128)S(1)} %cholesky.789), custom_call_target="Cholesky" | custom-call | tf_op jit(solution)/shard_map/jit(cholesky)/cholesky | solution.py:21
  628.2 9.8 custom-call.60
  641.3 11.9 %cholesky.606 = f32[128,128]{1,0:T(8,128)S(1)} custom-call(f32[128,128]{1,0:T(8,128)S(1)} %cholesky.793), custom_call_target="Cholesky" | custom-call | tf_op jit(solution)/shard_map/jit(cholesky)/cholesky | solution.py:21
  653.7 9.8 custom-call.61
  666.6 13.2 %cholesky.627 = f32[128,128]{1,0:T(8,128)} custom-call(f32[128,128]{1,0:T(8,128)} %cholesky.798), custom_call_target="Cholesky" | custom-call | tf_op jit(solution)/shard_map/jit(cholesky)/cholesky | solution.py:21
  681.8 11.5 %custom-call.62 = f32[1,128,128]{1,2,0:T(8,128)} custom-call(f32[1,128,128]{2,1,0:T(8,128)} %get-tuple-element.236), custom_call_target="InvertDiagBlocksLowerTriangular" | custom-call | tf_op jit(solution)/shard_map/jit(cholesky)/cholesky/custom-call.11 | solution.py:21
  695.6 11.7 %cholesky.640 = f32[128,128]{1,0:T(8,128)S(1)} custom-call(f32[128,128]{1,0:T(8,128)S(1)} %convolution_subtract_fusion.31), custom_call_target="Cholesky" | custom-call | tf_op jit(solution)/shard_map/jit(cholesky)/cholesky | solution.py:21
  715.6 11.5 %while.24 = (s32[]{:T(128)}, f32[512,512]{1,0:T(8,128)}, s32[4,2]{0,1:T(2,128)S(1)}, f32[4,128,128]{2,1,0:T(8,128)S(1)}, s32[]{:T(128)}) while((s32[]{:T(128)}, f32[512,512]{1,0:T(8,128)}, s32[4,2]{0,1:T(2,128)S(1)}, f32[4,128,128]{2,1,0:T(8,128)S(1)}, s32[]{:T(128)}) %tuple.232), condition=%wide.while_cond.3.clone, body=%wide.while_body.3.clone.sunk | while | flops 2 | bytes 131189 | solution.py:22
  727.1 40.3 %custom-call.63 = f32[4,128,128]{1,2,0:T(8,128)} custom-call(f32[4,128,128]{2,1,0:T(8,128)S(1)} %get-tuple-element.107), custom_call_target="InvertDiagBlocksLowerTriangular" | custom-call | tf_op jit(solution)/shard_map/jit(_solve_triangular)/triangular_solve | solution.py:22
  779.3 2.5 fusion.4
  783.4 6.9 all-gather.8.cloned.1.call-done
  792.5 10.9 while.28
  803.4 40.9 %custom-call.71 = f32[4,128,128]{1,2,0:T(8,128)} custom-call(f32[4,128,128]{2,1,0:T(8,128)} %get-tuple-element.111), custom_call_target="InvertDiagBlocksLowerTriangular" | custom-call | tf_op jit(solution)/shard_map/jit(_solve_triangular)/triangular_solve | solution.py:23
  852.0 11.7 %cholesky.750 = f32[128,128]{1,0:T(8,128)S(1)} custom-call(f32[128,128]{1,0:T(8,128)S(1)} %cholesky.818), custom_call_target="Cholesky" | custom-call | tf_op jit(solution)/shard_map/jit(cholesky)/cholesky | solution.py:26
  865.8 11.3 %custom-call.72 = f32[1,128,128]{1,2,0:T(8,128)} custom-call(f32[1,128,128]{2,1,0:T(8,128)} %get-tuple-element.232), custom_call_target="InvertDiagBlocksLowerTriangular" | custom-call | tf_op jit(solution)/shard_map/jit(cholesky)/cholesky/custom-call.11 | solution.py:26
  879.9 13.6 %cholesky.760 = f32[128,128]{1,0:T(8,128)} custom-call(f32[128,128]{1,0:T(8,128)} %convolution_subtract_fusion.27), custom_call_target="Cholesky" | custom-call | tf_op jit(solution)/shard_map/jit(cholesky)/cholesky | solution.py:26
  898.6 6.5 while.29
  905.1 21.1 %custom-call.73 = f32[2,128,128]{1,2,0:T(8,128)} custom-call(f32[2,128,128]{2,1,0:T(8,128)} %get-tuple-element.112), custom_call_target="InvertDiagBlocksLowerTriangular" | custom-call | tf_op jit(solution)/shard_map/jit(_solve_triangular)/triangular_solve | solution.py:28
  929.9 2.7 fusion.238
  936.4 11.7 %cholesky.682 = f32[128,128]{1,0:T(8,128)S(1)} custom-call(f32[128,128]{1,0:T(8,128)S(1)} %cholesky.805), custom_call_target="Cholesky" | custom-call | tf_op jit(solution)/shard_map/jit(cholesky)/cholesky | solution.py:21
  950.3 11.3 %custom-call.67 = f32[1,128,128]{1,2,0:T(8,128)} custom-call(f32[1,128,128]{2,1,0:T(8,128)} %get-tuple-element.228), custom_call_target="InvertDiagBlocksLowerTriangular" | custom-call | tf_op jit(solution)/shard_map/jit(cholesky)/cholesky | solution.py:21
  965.4 13.3 %cholesky.701 = f32[128,128]{1,0:T(8,128)} custom-call(f32[128,128]{1,0:T(8,128)} %cholesky.809), custom_call_target="Cholesky" | custom-call | tf_op jit(solution)/shard_map/jit(cholesky)/cholesky | solution.py:21
  980.8 11.3 %custom-call.68 = f32[1,128,128]{1,2,0:T(8,128)} custom-call(f32[1,128,128]{2,1,0:T(8,128)} %get-tuple-element.225), custom_call_target="InvertDiagBlocksLowerTriangular" | custom-call | tf_op jit(solution)/shard_map/jit(cholesky)/cholesky | solution.py:21
  995.8 13.2 %cholesky.722 = f32[128,128]{1,0:T(8,128)} custom-call(f32[128,128]{1,0:T(8,128)} %cholesky.814), custom_call_target="Cholesky" | custom-call | tf_op jit(solution)/shard_map/jit(cholesky)/cholesky | solution.py:21
  1011.0 11.4 %custom-call.69 = f32[1,128,128]{1,2,0:T(8,128)} custom-call(f32[1,128,128]{2,1,0:T(8,128)} %get-tuple-element.222), custom_call_target="InvertDiagBlocksLowerTriangular" | custom-call | tf_op jit(solution)/shard_map/jit(cholesky)/cholesky/custom-call.11 | solution.py:21
  1025.4 13.2 %cholesky.735 = f32[128,128]{1,0:T(8,128)} custom-call(f32[128,128]{1,0:T(8,128)} %convolution_subtract_fusion.30), custom_call_target="Cholesky" | custom-call | tf_op jit(solution)/shard_map/jit(cholesky)/cholesky | solution.py:21
  1047.0 11.6 %while.27 = (s32[]{:T(128)}, f32[512,512]{1,0:T(8,128)}, s32[4,2]{0,1:T(2,128)S(1)}, f32[4,128,128]{2,1,0:T(8,128)S(1)}, s32[]{:T(128)}) while((s32[]{:T(128)}, f32[512,512]{1,0:T(8,128)}, s32[4,2]{0,1:T(2,128)S(1)}, f32[4,128,128]{2,1,0:T(8,128)S(1)}, s32[]{:T(128)}) %tuple.234), condition=%wide.while_cond.3.clone.1, body=%wide.while_body.3.clone.1.sunk | while | flops 2 | bytes 131189 | solution.py:22
  1058.7 39.6 %custom-call.70 = f32[4,128,128]{1,2,0:T(8,128)S(1)} custom-call(f32[4,128,128]{2,1,0:T(8,128)S(1)} %get-tuple-element.110), custom_call_target="InvertDiagBlocksLowerTriangular" | custom-call | tf_op jit(solution)/shard_map/jit(_solve_triangular)/triangular_solve | solution.py:22
  1106.2 2.5 fusion.8
  (393 shorter events, 270.9 us)
Async XLA Ops:
  7.2 107.7 %all-reduce.5.cloned.1.call-start = ((), (), s32[]{:S(2)}) async-start(), calls=%async_computation.3 | async-start | bytes 3932160 | tf_op jit(solution)/shard_map/psum | solution.py:12
  8.3 2.6 copy-start.13
  11.8 124.0 %all-gather.4.cloned.1.call-start = ((), (), s32[]{:S(2)}) async-start(), calls=%async_computation | async-start | bytes 1966080 | tf_op jit(solution)/shard_map/all_gather | solution.py:52
  114.9 5.6 copy-start.32
  114.9 6.5 copy-start.25
  116.8 359.1 %all-gather.6.cloned.1.call-start = ((), (), s32[]{:S(2)}) async-start(), calls=%async_computation.1 | async-start | bytes 1966080 | tf_op jit(solution)/shard_map/all_gather | solution.py:52
  117.0 419.1 %copy-start.6 = (f32[256,256]{1,0:T(8,128)}, f32[256,256]{1,0:T(8,128)S(1)}, u32[]{:S(2)}) copy-start(f32[256,256]{1,0:T(8,128)S(1)} %copy.9) | copy-start | bytes 786436
  135.8 53.6 %copy-start = (f32[512,768]{1,0:T(8,128)S(1)}, f32[512,768]{1,0:T(8,128)}, u32[]{:S(2)}) copy-start(f32[512,768]{1,0:T(8,128)} %all-gather.4.cloned.1.call-done) | copy-start | bytes 4718596
  196.0 44.9 %copy-start.46 = (s32[2]{0:T(128)S(1)}, s32[2]{0:T(128)}, u32[]{:S(2)}) copy-start(s32[2]{0:T(128)} %iota_multiply_fusion) | copy-start | bytes 28
  198.8 0.7 copy-start.22
  246.5 0.5 copy-start.45
  266.7 0.7 copy-start.39
  278.4 1.0 copy-start.10
  311.7 0.7 copy-start.26
  342.9 0.7 copy-start.30
  456.1 334.2 %all-gather.8.cloned.1.call-start = ((), (), s32[]{:S(2)}) async-start(), calls=%async_computation.2 | async-start | bytes 1966080 | tf_op jit(solution)/shard_map/all_gather | solution.py:52
  457.9 1.4 copy-start.36
  464.3 1.0 copy-start.20
  465.2 4.0 copy-start.21
  465.2 4.0 copy-start.38
  467.8 3.1 copy-start.44
  475.9 53.6 %copy-start.1 = (f32[512,768]{1,0:T(8,128)S(1)}, f32[512,768]{1,0:T(8,128)}, u32[]{:S(2)}) copy-start(f32[512,768]{1,0:T(8,128)} %all-gather.6.cloned.1.call-done) | copy-start | bytes 4718596
  538.2 0.7 copy-start.23
  577.3 1.9 copy-start.17
  605.8 2.3 copy-start.40
  607.2 0.8 copy-start.4
  614.8 1.0 copy-start.11
  640.6 0.7 copy-start.27
  714.5 53.0 %copy-start.29 = (f32[128,256]{1,0:T(8,128)S(1)}, f32[128,256]{1,0:T(8,128)}, u32[]{:S(2)}) copy-start(f32[128,256]{1,0:T(8,128)} %fusion.47) | copy-start | bytes 393220
  715.6 54.1 %copy-start.19 = (f32[128,512]{1,0:T(8,128)S(1)}, f32[128,512]{1,0:T(8,128)}, u32[]{:S(2)}) copy-start(f32[128,512]{1,0:T(8,128)} %get-tuple-element.209) | copy-start | bytes 786436
  767.5 4.4 copy-start.5
  767.5 4.4 copy-start.8
  771.9 1.4 copy-start.37
  778.2 0.9 copy-start.14
  778.2 1.0 copy-start.15
  779.3 4.1 copy-start.43
  790.3 54.0 %copy-start.2 = (f32[512,768]{1,0:T(8,128)S(1)}, f32[512,768]{1,0:T(8,128)}, u32[]{:S(2)}) copy-start(f32[512,768]{1,0:T(8,128)} %all-gather.8.cloned.1.call-done) | copy-start | bytes 4718596
  844.3 2.9 copy-start.33
  847.6 1.8 copy-start.7
  851.3 0.7 copy-start.24
  863.7 0.6 copy-start.34
  895.0 2.0 copy-start.18
  926.2 2.2 copy-start.41
  935.4 1.0 copy-start.12
  948.1 0.6 copy-start.35
  964.1 0.7 copy-start.28
  994.5 0.7 copy-start.31
  1105.0 1.1 copy-start.9
  1105.0 1.2 copy-start.16
  1106.2 2.6 copy-start.42
  1108.8 0.9 copy-start.3
Sparse Core Ops, SparseCore 0:
  12.9 101.9 all-reduce.4
  117.0 18.7 all-gather.3
  456.2 19.6 all-gather.5
  770.6 19.6 all-gather.7
where the time goes:
time: 1120 us
  other arithmetic  731 us (65%)
  waiting for transfers between devices  128 us (11%)
  local copies, waits for them, and re-layouts  125 us (11%)
  matrix products  105 us (9%)
  between operations  26.8 us (2%)
    another operation x44, other arithmetic, transform(): new_diag = jnp.linalg.cholesky(gram_matrix)  280 us
    another operation x6, other arithmetic, transform(): jax.scipy.linalg.solve_triangular(diag_block, v_block, lower=True)  126 us
    another operation x7, other arithmetic, transform(): leading = jax.scipy.linalg.solve_triangular(new_diag, stacked, lower=True)  125 us
    another operation x20, other arithmetic, transform(): lower_inner = jnp.linalg.cholesky(inner_gram)  111 us
    psum x1, waiting for transfers between devices, spread(): return lax.psum(block, axis)  103 us
    another operation x7, other arithmetic, transform(): jax.scipy.linalg.solve_triangular(lower_inner, null_basis.T, lower=True)  65.2 us
    another operation x43, local copies, waits for them, and re-layouts, transform(): leading = jax.scipy.linalg.solve_triangular(new_diag, stacked, lower=True)  38.1 us
    another operation x36, local copies, waits for them, and re-layouts, transform(): jax.scipy.linalg.solve_triangular(diag_block, v_block, lower=True)  33.9 us
  transfers between devices with their start and end apart: 4, of which 4 were waited for; matrix products, arithmetic and copies ran while one was open for 3% of the time, Pallas kernels for 0%

commit v1 on v0

--- a/solution.py
+++ b/solution.py
@@ -8,8 +8,12 @@
 
 
 def spread(block, axis, owner):
+
+    def finish_keys_over_axis(local, shard_axis):
+        return lax.all_gather(local, shard_axis).sum(axis=0)
+
     block = jnp.where(lax.axis_index(axis) == owner, block, jnp.zeros_like(block))
-    return lax.psum(block, axis)
+    return finish_keys_over_axis(block, axis)
 
 
 def transform(stacked):

time: 1120 us -> 1180 us (1.054)
  waiting for transfers between devices: 128 us -> 207 us
  other arithmetic: 731 us -> 713 us
    all_gather x0 -> x6, waiting for transfers between devices: none -> 164 us  [finish_keys_over_axis(): return lax.all_gather(local, shard_axis).sum(axis=0)]
    psum x1 -> x0, waiting for transfers between devices: 103 us -> none  [spread(): return lax.psum(block, axis)]
    another operation x44, other arithmetic: 280 us -> 252 us  [transform(): new_diag = jnp.linalg.cholesky(gram_matrix)]
    all_gather x3, waiting for transfers between devices: 24.8 us -> 42.1 us  [on_device(): diag_rows = lax.all_gather(current, 'depth', axis=0, tiled=True)]
    reduce_sum x0 -> x6, other arithmetic: none -> 13.2 us  [finish_keys_over_axis(): return lax.all_gather(local, shard_axis).sum(axis=0)]
  transfers between devices with their start and end apart: 4 -> 9, of which waited for: 4 -> 7; matrix products, arithmetic and copies ran while one was open for 3% -> 51% of each run, Pallas kernels for 0% -> 0%
where the time goes in v1:
time: 1180 us; the launch traced here: 1170 us
  other arithmetic  713 us (60%)
  waiting for transfers between devices  207 us (18%)
  local copies, waits for them, and re-layouts  119 us (10%)
  matrix products  99.7 us (8%)
  between operations  27 us (2%)
    another operation x44, other arithmetic, transform(): new_diag = jnp.linalg.cholesky(gram_matrix)  252 us
    all_gather x6, waiting for transfers between devices, finish_keys_over_axis(): return lax.all_gather(local, shard_axis).sum(axis=0)  164 us
    another operation x6, other arithmetic, transform(): jax.scipy.linalg.solve_triangular(diag_block, v_block, lower=True)  125 us
    another operation x7, other arithmetic, transform(): leading = jax.scipy.linalg.solve_triangular(new_diag, stacked, lower=True)  125 us
    another operation x20, other arithmetic, transform(): lower_inner = jnp.linalg.cholesky(inner_gram)  113 us
    another operation x7, other arithmetic, transform(): jax.scipy.linalg.solve_triangular(lower_inner, null_basis.T, lower=True)  64.5 us
    all_gather x3, waiting for transfers between devices, on_device(): diag_rows = lax.all_gather(current, 'depth', axis=0, tiled=True)  42.1 us
    another operation x43, local copies, waits for them, and re-layouts, transform(): leading = jax.scipy.linalg.solve_triangular(new_diag, stacked, lower=True)  38.9 us
  transfers between devices with their start and end apart: 9, of which 7 were waited for; matrix products, arithmetic and copies ran while one was open for 51% of the time, Pallas kernels for 0%

profile of v1, /device:TPU:0, one launch (start us, length us, event | category | flops | bytes accessed | tf_op | source)
XLA Modules:
  0.0 1165.5 jit_solution(6988690271727824718)
XLA Ops:
  10.1 43.7 %all-gather.24.cloned.1.call-done = f32[1024,256]{1,0:T(8,128)} async-done(((f32[128,256]{1,0:T(8,128)}), f32[1024,256]{1,0:T(8,128)}) %all-gather.24.cloned.1.call-update) | async-done | bytes 1048592 | tf_op jit(solution)/shard_map/all_gather | solution.py:13
  55.0 49.2 %all-gather.22.cloned.1.call-done = f32[1024,512]{1,0:T(8,128)} async-done(((f32[128,512]{1,0:T(8,128)}), f32[1024,512]{1,0:T(8,128)}) %all-gather.22.cloned.1.call-update) | async-done | bytes 2097168 | tf_op jit(solution)/shard_map/all_gather | solution.py:13
  109.3 15.9 %all-gather.16.cloned.1.call-done = f32[512,768]{1,0:T(8,128)} async-done(((f32[128,768]{1,0:T(8,128)}), f32[512,768]{1,0:T(8,128)}) %all-gather.16.cloned.1.call-update) | async-done | bytes 1572880 | tf_op jit(solution)/shard_map/all_gather | solution.py:56
  125.2 4.6 fusion.236
  131.4 11.7 %cholesky.492 = f32[128,128]{1,0:T(8,128)S(1)} custom-call(f32[128,128]{1,0:T(8,128)S(1)} %cholesky.773), custom_call_target="Cholesky" | custom-call | tf_op jit(solution)/shard_map/jit(cholesky)/cholesky | solution.py:25
  143.1 9.8 custom-call.53
  155.6 11.9 %cholesky.511 = f32[128,128]{1,0:T(8,128)S(1)} custom-call(f32[128,128]{1,0:T(8,128)S(1)} %cholesky.777), custom_call_target="Cholesky" | custom-call | tf_op jit(solution)/shard_map/jit(cholesky)/cholesky | solution.py:25
  167.5 9.8 custom-call.54
  178.9 11.7 %cholesky.532 = f32[128,128]{1,0:T(8,128)S(1)} custom-call(f32[128,128]{1,0:T(8,128)S(1)} %cholesky.782), custom_call_target="Cholesky" | custom-call | tf_op jit(solution)/shard_map/jit(cholesky)/cholesky | solution.py:25
  191.3 9.8 custom-call.55
  202.5 11.9 %cholesky.545 = f32[128,128]{1,0:T(8,128)S(1)} custom-call(f32[128,128]{1,0:T(8,128)S(1)} %convolution_subtract_fusion.32), custom_call_target="Cholesky" | custom-call | tf_op jit(solution)/shard_map/jit(cholesky)/cholesky | solution.py:25
  219.9 13.6 %while.21 = (s32[]{:T(128)}, f32[512,512]{1,0:T(8,128)}, s32[4,2]{0,1:T(2,128)S(1)}, f32[4,128,128]{2,1,0:T(8,128)}, s32[]{:T(128)}) while((s32[]{:T(128)}, f32[512,512]{1,0:T(8,128)}, s32[4,2]{0,1:T(2,128)S(1)}, f32[4,128,128]{2,1,0:T(8,128)}, s32[]{:T(128)}) %tuple.201), condition=%wide.while_cond.3, body=%wide.while_body.3.sunk | while | flops 2 | bytes 132705 | solution.py:26
  220.5 2.8 bitcast_dynamic-update-slice_fusion.18
  223.9 2.8 bitcast_dynamic-update-slice_fusion.18
  227.4 2.8 bitcast_dynamic-update-slice_fusion.18
  230.8 2.7 bitcast_dynamic-update-slice_fusion.18
  234.4 10.2 while.22
  244.6 40.7 %custom-call.56 = f32[4,128,128]{1,2,0:T(8,128)} custom-call(f32[4,128,128]{2,1,0:T(8,128)} %get-tuple-element.104), custom_call_target="InvertDiagBlocksLowerTriangular" | custom-call | tf_op jit(solution)/shard_map/jit(_solve_triangular)/triangular_solve | solution.py:26
  285.3 41.1 %custom-call.57 = f32[4,128,128]{1,2,0:T(8,128)} custom-call(f32[4,128,128]{2,1,0:T(8,128)} %get-tuple-element.105), custom_call_target="InvertDiagBlocksLowerTriangular" | custom-call | tf_op jit(solution)/shard_map/jit(_solve_triangular)/triangular_solve | solution.py:27
  332.4 11.7 %cholesky.560 = f32[128,128]{1,0:T(8,128)S(1)} custom-call(f32[128,128]{1,0:T(8,128)S(1)} %cholesky.786), custom_call_target="Cholesky" | custom-call | tf_op jit(solution)/shard_map/jit(cholesky)/cholesky | solution.py:30
  344.1 9.8 custom-call.58
  356.2 11.9 %cholesky.570 = f32[128,128]{1,0:T(8,128)S(1)} custom-call(f32[128,128]{1,0:T(8,128)S(1)} %convolution_subtract_fusion.29), custom_call_target="Cholesky" | custom-call | tf_op jit(solution)/shard_map/jit(cholesky)/cholesky | solution.py:30
  370.2 4.0 while.23
  374.9 20.3 %custom-call.59 = f32[2,128,128]{1,2,0:T(8,128)} custom-call(f32[2,128,128]{2,1,0:T(8,128)S(1)} %get-tuple-element.106), custom_call_target="InvertDiagBlocksLowerTriangular" | custom-call | tf_op jit(solution)/shard_map/jit(_solve_triangular)/triangular_solve | solution.py:32
  410.8 2.6 reduce_sum.56
  413.4 37.1 %all-gather.28.cloned.1.call-done = f32[1024,256]{1,0:T(8,128)} async-done(((f32[128,256]{1,0:T(8,128)}), f32[1024,256]{1,0:T(8,128)}) %all-gather.28.cloned.1.call-update) | async-done | bytes 1048592 | tf_op jit(solution)/shard_map/all_gather | solution.py:13
  458.3 33.8 %all-gather.32.cloned.1.call-done = f32[1024,256]{1,0:T(8,128)} async-done(((f32[128,256]{1,0:T(8,128)}), f32[1024,256]{1,0:T(8,128)}) %all-gather.32.cloned.1.call-update) | async-done | bytes 1048592 | tf_op jit(solution)/shard_map/all_gather | solution.py:13
  494.1 18.0 %all-gather.18.cloned.1.call-done = f32[512,768]{1,0:T(8,128)} async-done(((f32[128,768]{1,0:T(8,128)}), f32[512,768]{1,0:T(8,128)}) %all-gather.18.cloned.1.call-update) | async-done | bytes 1572880 | tf_op jit(solution)/shard_map/all_gather | solution.py:56
  512.1 4.7 fusion.237
  520.7 11.7 %cholesky.587 = f32[128,128]{1,0:T(8,128)S(1)} custom-call(f32[128,128]{1,0:T(8,128)S(1)} %cholesky.789), custom_call_target="Cholesky" | custom-call | tf_op jit(solution)/shard_map/jit(cholesky)/cholesky | solution.py:25
  533.6 9.8 custom-call.60
  546.6 11.9 %cholesky.606 = f32[128,128]{1,0:T(8,128)S(1)} custom-call(f32[128,128]{1,0:T(8,128)S(1)} %cholesky.793), custom_call_target="Cholesky" | custom-call | tf_op jit(solution)/shard_map/jit(cholesky)/cholesky | solution.py:25
  559.1 9.8 custom-call.61
  571.3 11.7 %cholesky.627 = f32[128,128]{1,0:T(8,128)S(1)} custom-call(f32[128,128]{1,0:T(8,128)S(1)} %cholesky.798), custom_call_target="Cholesky" | custom-call | tf_op jit(solution)/shard_map/jit(cholesky)/cholesky | solution.py:25
  583.7 9.8 custom-call.62
  595.8 11.9 %cholesky.640 = f32[128,128]{1,0:T(8,128)S(1)} custom-call(f32[128,128]{1,0:T(8,128)S(1)} %convolution_subtract_fusion.31), custom_call_target="Cholesky" | custom-call | tf_op jit(solution)/shard_map/jit(cholesky)/cholesky | solution.py:25
  616.1 11.6 while.24
  627.7 39.9 %custom-call.63 = f32[4,128,128]{1,2,0:T(8,128)} custom-call(f32[4,128,128]{2,1,0:T(8,128)S(1)} %get-tuple-element.107), custom_call_target="InvertDiagBlocksLowerTriangular" | custom-call | tf_op jit(solution)/shard_map/jit(_solve_triangular)/triangular_solve | solution.py:26
  668.8 11.6 while.25
  681.2 40.5 %custom-call.64 = f32[4,128,128]{1,2,0:T(8,128)S(1)} custom-call(f32[4,128,128]{2,1,0:T(8,128)} %copy-done.39), custom_call_target="InvertDiagBlocksLowerTriangular" | custom-call | tf_op jit(solution)/shard_map/jit(_solve_triangular)/triangular_solve | solution.py:27
  735.8 11.7 %cholesky.655 = f32[128,128]{1,0:T(8,128)S(1)} custom-call(f32[128,128]{1,0:T(8,128)S(1)} %cholesky.802), custom_call_target="Cholesky" | custom-call | tf_op jit(solution)/shard_map/jit(cholesky)/cholesky | solution.py:30
  748.8 10.4 custom-call.65
  762.0 11.7 %cholesky.665 = f32[128,128]{1,0:T(8,128)S(1)} custom-call(f32[128,128]{1,0:T(8,128)S(1)} %convolution_subtract_fusion.28), custom_call_target="Cholesky" | custom-call | tf_op jit(solution)/shard_map/jit(cholesky)/cholesky | solution.py:30
  779.2 7.0 while.26
  786.2 20.4 %custom-call.66 = f32[2,128,128]{1,2,0:T(8,128)} custom-call(f32[2,128,128]{2,1,0:T(8,128)S(1)} %get-tuple-element.109), custom_call_target="InvertDiagBlocksLowerTriangular" | custom-call | tf_op jit(solution)/shard_map/jit(_solve_triangular)/triangular_solve | solution.py:32
  812.6 4.2 reduce_sum.58
  832.3 8.3 all-gather.20.cloned.1.call-done
  842.8 10.5 while.28
  853.3 41.1 %custom-call.71 = f32[4,128,128]{1,2,0:T(8,128)} custom-call(f32[4,128,128]{2,1,0:T(8,128)} %get-tuple-element.111), custom_call_target="InvertDiagBlocksLowerTriangular" | custom-call | tf_op jit(solution)/shard_map/jit(_solve_triangular)/triangular_solve | solution.py:27
  900.9 2.7 fusion.238
  907.4 11.7 %cholesky.682 = f32[128,128]{1,0:T(8,128)S(1)} custom-call(f32[128,128]{1,0:T(8,128)S(1)} %cholesky.805), custom_call_target="Cholesky" | custom-call | tf_op jit(solution)/shard_map/jit(cholesky)/cholesky | solution.py:25
  921.4 11.4 custom-call.67
  936.6 13.2 %cholesky.701 = f32[128,128]{1,0:T(8,128)} custom-call(f32[128,128]{1,0:T(8,128)} %cholesky.809), custom_call_target="Cholesky" | custom-call | tf_op jit(solution)/shard_map/jit(cholesky)/cholesky | solution.py:25
  952.7 11.3 custom-call.68
  967.7 13.2 %cholesky.722 = f32[128,128]{1,0:T(8,128)} custom-call(f32[128,128]{1,0:T(8,128)} %cholesky.814), custom_call_target="Cholesky" | custom-call | tf_op jit(solution)/shard_map/jit(cholesky)/cholesky | solution.py:25
  983.0 11.5 custom-call.69
  997.4 13.2 %cholesky.735 = f32[128,128]{1,0:T(8,128)} custom-call(f32[128,128]{1,0:T(8,128)} %convolution_subtract_fusion.30), custom_call_target="Cholesky" | custom-call | tf_op jit(solution)/shard_map/jit(cholesky)/cholesky | solution.py:25
  1015.8 11.6 while.27
  1027.4 39.7 %custom-call.70 = f32[4,128,128]{1,2,0:T(8,128)S(1)} custom-call(f32[4,128,128]{2,1,0:T(8,128)S(1)} %get-tuple-element.110), custom_call_target="InvertDiagBlocksLowerTriangular" | custom-call | tf_op jit(solution)/shard_map/jit(_solve_triangular)/triangular_solve | solution.py:26
  1075.7 13.2 %cholesky.750 = f32[128,128]{1,0:T(8,128)} custom-call(f32[128,128]{1,0:T(8,128)} %cholesky.818), custom_call_target="Cholesky" | custom-call | tf_op jit(solution)/shard_map/jit(cholesky)/cholesky | solution.py:30
  1091.2 11.3 custom-call.72
  1105.3 13.3 %cholesky.760 = f32[128,128]{1,0:T(8,128)} custom-call(f32[128,128]{1,0:T(8,128)} %convolution_subtract_fusion.27), custom_call_target="Cholesky" | custom-call | tf_op jit(solution)/shard_map/jit(cholesky)/cholesky | solution.py:30
  1123.8 6.7 while.29
  1130.6 21.1 %custom-call.73 = f32[2,128,128]{1,2,0:T(8,128)} custom-call(f32[2,128,128]{2,1,0:T(8,128)} %get-tuple-element.112), custom_call_target="InvertDiagBlocksLowerTriangular" | custom-call | tf_op jit(solution)/shard_map/jit(_solve_triangular)/triangular_solve | solution.py:32
  (415 shorter events, 253.7 us)
Async XLA Ops:
  7.2 1.2 copy-start.17
  7.2 46.5 %all-gather.24.cloned.1.call-start = ((), (), s32[]{:S(2)}) async-start(), calls=%async_computation.4 | async-start | bytes 1179648 | tf_op jit(solution)/shard_map/all_gather | solution.py:13
  9.1 95.2 %all-gather.22.cloned.1.call-start = ((), (), s32[]{:S(2)}) async-start(), calls=%async_computation.3 | async-start | bytes 2359296 | tf_op jit(solution)/shard_map/all_gather | solution.py:13
  10.0 115.2 %all-gather.16.cloned.1.call-start = ((), (), s32[]{:S(2)}) async-start(), calls=%async_computation | async-start | bytes 1966080 | tf_op jit(solution)/shard_map/all_gather | solution.py:56
  106.9 303.9 %all-gather.26.cloned.1.call-start = ((), (), s32[]{:S(2)}) async-start(), calls=%async_computation.5 | async-start | bytes 4718592 | tf_op jit(solution)/shard_map/all_gather | solution.py:13
  107.8 342.8 %all-gather.28.cloned.1.call-start = ((), (), s32[]{:S(2)}) async-start(), calls=%async_computation.6 | async-start | bytes 1179648 | tf_op jit(solution)/shard_map/all_gather | solution.py:13
  130.4 1.0 copy-start.11
  218.1 15.4 %copy-start.1 = (f32[512,768]{1,0:T(8,128)S(1)}, f32[512,768]{1,0:T(8,128)}, u32[]{:S(2)}) copy-start(f32[512,768]{1,0:T(8,128)} %all-gather.16.cloned.1.call-done) | copy-start | bytes 4718596
  326.4 3.0 copy-start.35
  329.1 1.4 copy-start.14
  329.7 0.7 copy-start.20
  330.5 0.7 copy-start.33
  332.3 11.8 %copy-start.27 = (f32[256,256]{1,0:T(8,128)}, f32[256,256]{1,0:T(8,128)S(1)}, u32[]{:S(2)}) copy-start(f32[256,256]{1,0:T(8,128)S(1)} %fusion.117) | copy-start | bytes 786436
  332.3 62.8 %copy-start.15 = (f32[128,256]{1,0:T(8,128)S(1)}, f32[128,256]{1,0:T(8,128)}, u32[]{:S(2)}) copy-start(f32[128,256]{1,0:T(8,128)} %copy-done.14) | copy-start | bytes 393220
  332.3 62.8 %copy-start.21 = (f32[128,256]{1,0:T(8,128)S(1)}, f32[128,256]{1,0:T(8,128)}, u32[]{:S(2)}) copy-start(f32[128,256]{1,0:T(8,128)} %copy-done.20) | copy-start | bytes 393220
  353.9 42.2 %copy-start.6 = (f32[256,256]{1,0:T(8,128)S(1)}, f32[256,256]{1,0:T(8,128)}, u32[]{:S(2)}) copy-start(f32[256,256]{1,0:T(8,128)} %copy.9) | copy-start | bytes 786436
  374.1 0.7 copy-start.16
  374.2 0.7 copy-start.47
  395.1 1.1 copy-start.42
  396.7 2.3 copy-start.41
  398.9 52.9 %copy-start.4 = (f32[128,768]{1,0:T(8,128)}, f32[128,768]{1,0:T(8,128)S(1)}, u32[]{:S(2)}) copy-start(f32[128,768]{1,0:T(8,128)S(1)} %fusion.179) | copy-start | bytes 1179652
  405.8 0.9 copy-start.18
  405.8 1.0 copy-start.26
  410.1 82.0 %all-gather.32.cloned.1.call-start = ((), (), s32[]{:S(2)}) async-start(), calls=%async_computation.8 | async-start | bytes 1179648 | tf_op jit(solution)/shard_map/all_gather | solution.py:13
  410.7 101.4 %all-gather.18.cloned.1.call-start = ((), (), s32[]{:S(2)}) async-start(), calls=%async_computation.1 | async-start | bytes 1966080 | tf_op jit(solution)/shard_map/all_gather | solution.py:56
  453.6 358.9 %all-gather.30.cloned.1.call-start = ((), (), s32[]{:S(2)}) async-start(), calls=%async_computation.7 | async-start | bytes 7077888 | tf_op jit(solution)/shard_map/all_gather | solution.py:13
  454.7 385.9 %all-gather.20.cloned.1.call-start = ((), (), s32[]{:S(2)}) async-start(), calls=%async_computation.2 | async-start | bytes 1966080 | tf_op jit(solution)/shard_map/all_gather | solution.py:56
  519.6 1.1 copy-start.12
  613.5 54.1 %copy-start = (f32[512,768]{1,0:T(8,128)S(1)}, f32[512,768]{1,0:T(8,128)}, u32[]{:S(2)}) copy-start(f32[512,768]{1,0:T(8,128)} %all-gather.18.cloned.1.call-done) | copy-start | bytes 4718596
  680.4 0.7 copy-start.39
  721.7 0.7 copy-start.36
  729.8 0.7 copy-start.34
  735.0 0.7 copy-start.28
  806.7 1.1 copy-start.43
  816.8 1.3 copy-start.5
  816.8 1.3 copy-start.31
  816.8 2.2 copy-start.8
  819.0 1.8 copy-start.9
  820.8 1.4 copy-start.40
  827.1 0.9 copy-start.19
  827.1 1.0 copy-start.22
  828.1 4.1 copy-start.46
  840.6 53.8 %copy-start.2 = (f32[512,768]{1,0:T(8,128)S(1)}, f32[512,768]{1,0:T(8,128)}, u32[]{:S(2)}) copy-start(f32[512,768]{1,0:T(8,128)} %all-gather.20.cloned.1.call-done) | copy-start | bytes 4718596
  894.4 2.9 copy-start.37
  906.4 1.0 copy-start.10
  919.1 0.6 copy-start.38
  935.3 0.7 copy-start.30
  966.4 0.7 copy-start.32
  1073.9 1.0 copy-start.24
  1075.0 13.8 %copy-start.29 = (f32[256,256]{1,0:T(8,128)}, f32[256,256]{1,0:T(8,128)S(1)}, u32[]{:S(2)}) copy-start(f32[256,256]{1,0:T(8,128)S(1)} %fusion.115) | copy-start | bytes 786436
  1075.0 76.6 %copy-start.7 = (f32[256,256]{1,0:T(8,128)S(1)}, f32[256,256]{1,0:T(8,128)}, u32[]{:S(2)}) copy-start(f32[256,256]{1,0:T(8,128)} %copy.9) | copy-start | bytes 786436
  1075.0 76.6 %copy-start.13 = (f32[512,256]{1,0:T(8,128)S(1)}, f32[512,256]{1,0:T(8,128)}, u32[]{:S(2)}) copy-start(f32[512,256]{1,0:T(8,128)} %fusion.95) | copy-start | bytes 1572868
  1119.5 2.7 copy-start.25
  1151.7 0.9 copy-start.44
  1153.1 1.4 copy-start.23
  1154.5 2.5 copy-start.45
  1157.9 0.9 copy-start.3
Sparse Core Ops, SparseCore 0:
  10.7 42.9 all-gather.23
  56.4 47.7 all-gather.21
  107.0 18.1 all-gather.15
  127.7 73.0 all-gather.25
  410.2 40.2 all-gather.27
  453.1 38.9 all-gather.31
  493.7 18.3 all-gather.17
  514.8 98.9 all-gather.29
  820.9 19.6 all-gather.19
